TPU v7x, 256 devices: a whole 4x4x8 slice. The times are simulated.
256 devices in a mesh: worker: 16 (over x_lo, y, core), mp: 16 (over x_hi, z).
Axes of the slice: x: 4 (x_hi: 2, x_lo: 2; x = x_hi * 2 + x_lo), y: 4, z: 8, core: 2. Of those that a mesh axis runs over, the one named last changes fastest.
Arguments:
- grad: bfloat16 [16, 2048, 14336], P('worker', 'mp'), may hold values from -24 to 24
Outputs:
- median: bfloat16 [2048, 14336], P('mp')
- trimmed: bfloat16 [2048, 14336], P('mp')
All inputs are finite; a program needn't handle non-finite values.
Results may differ from a plain program's by a relative error of at most 0.0048.
Values may be sent and summed in bfloat16 or wider, within the bound.
No kernel may reach another device: no remote copies, remote signals or barrier semaphores. Data moves between devices by JAX's collectives and lax.ppermute only.
A program may use at most 64 MiB of HBM per device.

v0:
```python
import jax
import jax.numpy as jnp
from jax import lax
from jax.sharding import PartitionSpec as P


def from_everyone(array, axis):
    count = lax.axis_size(axis)
    return lax.all_to_all(
        jnp.broadcast_to(array[None], (count, *array.shape)), axis, 0, 0, tiled=True
    )


def over_copies(array, axis):
    return from_everyone(array, axis).sum(axis=0)


def in_order(pieces, dim):
    shape = list(pieces.shape[1:])
    shape[dim] *= pieces.shape[0]
    return jnp.moveaxis(pieces, 0, dim).reshape(shape)


def gather_directly(array, axis, dim):
    return in_order(from_everyone(array, axis), dim)


def side_by_side(arrays, axis, dim, along):
    both = jnp.concatenate(arrays, axis=along)
    result, at, gathered = (lax.all_gather(both, axis, axis=dim, tiled=True), 0, [])
    for a in arrays:
        gathered.append(lax.slice_in_dim(result, at, at + a.shape[along], axis=along))
        at += a.shape[along]
    return tuple(gathered)


def sort_copies(stacked):
    copies = stacked.shape[0]
    rest = stacked.shape[1:]
    span_size = 2
    while span_size <= copies:
        step_size = span_size // 2
        while step_size >= 1:
            if span_size == copies:
                grouped = stacked.reshape((copies // (2 * step_size), 2, step_size) + rest)
                lowest = jnp.minimum(grouped[:, 0], grouped[:, 1])
                highest = jnp.maximum(grouped[:, 0], grouped[:, 1])
                stacked = jnp.stack([lowest, highest], axis=1).reshape(stacked.shape)
            else:
                grouped = stacked.reshape(
                    (copies // (2 * span_size), 2, span_size // (2 * step_size), 2, step_size)
                    + rest
                )
                lowest = jnp.minimum(grouped[:, :, :, 0], grouped[:, :, :, 1])
                highest = jnp.maximum(grouped[:, :, :, 0], grouped[:, :, :, 1])
                rising = jnp.stack([lowest[:, 0], highest[:, 0]], axis=2)
                falling = jnp.stack([highest[:, 1], lowest[:, 1]], axis=2)
                stacked = jnp.stack([rising, falling], axis=1).reshape(stacked.shape)
            step_size = step_size // 2
        span_size = span_size * 2
    return stacked


def summarize(stacked):
    ordered = sort_copies(stacked)
    copies = ordered.shape[0]
    middle = copies // 2
    trim_count = copies // 4
    median = (
        (ordered[middle - 1].astype(jnp.float32) + ordered[middle].astype(jnp.float32)) * 0.5
    ).astype(jnp.bfloat16)
    kept = jnp.sum(ordered[trim_count : copies - trim_count].astype(jnp.float32), axis=0) / (
        copies - 2 * trim_count
    )
    return (median, kept.astype(jnp.bfloat16))


def shards(grad):
    partial_power = jnp.sum(jnp.square(grad.astype(jnp.float32)))
    power = over_copies(partial_power, "mp")
    total_cells = grad.shape[1] * lax.axis_size("mp") * grad.shape[2]
    factor = lax.rsqrt(power / total_cells + 0.25)
    factors = gather_directly(factor.reshape(1), "worker", 0)
    scaled = (
        lax.all_to_all(grad, "worker", split_axis=1, concat_axis=0, tiled=True).astype(jnp.float32)
        * factors[:, None, None]
    ).astype(jnp.bfloat16)
    median, trimmed = summarize(scaled)
    median, trimmed = side_by_side((median, trimmed), "worker", 0, 1)
    return (median, trimmed)


def solution(mesh):
    return jax.shard_map(
        shards,
        mesh=mesh,
        in_specs=(P("worker", "mp", None),),
        out_specs=(P("mp", None), P("mp", None)),
        check_vma=False,
    )
```

profile of v0, /device:TPU:1, one launch (start us, length us, event | category | flops | bytes accessed | tf_op | source)
XLA Modules:
  0.0 228.6 jit_solution(8920041473013711505)
XLA Ops:
  7.2 4.5 %multiply_reduce_fusion = f32[]{:T(128)} fusion(bf16[1,128,14336]{2,1,0:T(8,128)(2,1)} %param.1), kind=kLoop, calls=%fused_computation.2 | loop fusion | flops 5505023 | bytes 3670020 | tf_op jit(solution)/shard_map/reduce_sum | solution.py:79
  11.7 1.2 broadcast_in_dim.4
  12.9 11.6 %all-to-all-start.1 = ((f32[16,1,1]{2,1,0:T(1,128)}), f32[16,1,1]{2,1,0:T(1,128)S(1)}, u32[]{:S(2)}, u32[]{:S(2)}) async-start(f32[16,1,1]{2,1,0:T(1,128)} %broadcast_in_dim.4), calls=%async_computation.1 | async-start | bytes 16384 | tf_op jit(solution)/shard_map/all_to_all | solution.py:9
  24.5 7.8 %copy.158 = bf16[1,128,14336]{2,0,1:T(2,128)(2,1)} copy(bf16[1,128,14336]{2,1,0:T(8,128)(2,1)} %param.1) | data formatting | bytes 7340032 | tf_op args[0]
  32.3 0.6 broadcast.17
  32.9 23.8 %reduce.3 = bf16[128,14336]{1,0:T(8,128)(2,1)} reduce(bf16[128,1,14336]{2,1,0:T(2,128)(2,1)} %bitcast.115, bf16[]{:T(256)} %broadcast.17), dimensions={1}, to_apply=%bitcast.114.reduce_sub_computation | reduce | bytes 7340034
  56.7 0.6 reduce_sum.28
  58.0 0.6 broadcast_in_dim.5
  58.6 5.5 %all-to-all-start.2 = ((f32[16,1,1]{2,1,0:T(1,128)}), f32[16,1,1]{2,1,0:T(1,128)S(1)}, u32[]{:S(2)}, u32[]{:S(2)}) async-start(f32[16,1,1]{2,1,0:T(1,128)} %broadcast_in_dim.5), calls=%async_computation.2 | async-start | bytes 16384 | tf_op jit(solution)/shard_map/all_to_all | solution.py:9
  64.1 11.6 %reshape.391 = bf16[16,2,57344]{2,1,0:T(2,128)(2,1)} reshape(bf16[128,14336]{1,0:T(8,128)(2,1)} %reduce.3) | data formatting | bytes 7340032
  75.7 5.7 %all-to-all-start = ((bf16[16,2,57344]{2,1,0:T(2,128)(2,1)}), bf16[16,2,57344]{2,1,0:T(2,128)(2,1)}, u32[]{:S(2)}, u32[]{:S(2)}) async-start(bf16[16,2,57344]{2,1,0:T(2,128)(2,1)} %reshape.391), calls=%async_computation | async-start | bytes 7340032 | tf_op jit(solution)/shard_map/all_to_all | solution.py:85
  81.4 0.2 all-gather.2.cloned.1.call-start
  81.6 0.2 reduce.2
  81.8 0.1 mul.24
  81.9 48.0 %all-to-all-done = bf16[16,2,57344]{2,1,0:T(2,128)(2,1)} async-done(((bf16[16,2,57344]{2,1,0:T(2,128)(2,1)}), bf16[16,2,57344]{2,1,0:T(2,128)(2,1)}, u32[]{:S(2)}, u32[]{:S(2)}) %all-to-all-start) | async-done | bytes 3670048 | tf_op jit(solution)/shard_map/all_to_all | solution.py:85
  129.9 12.0 %reshape.392 = bf16[128,1,14336]{2,1,0:T(2,128)(2,1)} reshape(bf16[16,2,57344]{2,1,0:T(2,128)(2,1)} %all-to-all-done) | data formatting | bytes 7340032
  141.9 5.2 %copy.123 = bf16[1,128,14336]{2,1,0:T(8,128)(2,1)S(1)} copy(bf16[1,128,14336]{2,0,1:T(2,128)(2,1)} %bitcast.116) | data formatting | bytes 7340032 | tf_op jit(solution)/shard_map/all_to_all | solution.py:85
  147.0 0.7 fusion
  147.8 0.2 fusion.9
  148.0 0.2 maximum_bitcast_fusion.4
  148.2 0.2 fusion.24
  148.4 0.3 fusion.14
  148.7 0.1 copy.130
  148.9 0.1 slice_bitcast_fusion.12
  149.0 0.1 copy.128
  149.1 0.1 slice_bitcast_fusion.13
  149.3 0.2 maximum_bitcast_fusion.1
  149.4 0.2 maximum_bitcast_fusion.2
  149.6 0.3 maximum_bitcast_fusion
  150.0 0.2 fusion.8
  150.2 0.2 fusion.16
  150.5 0.1 slice_bitcast_fusion.11
  150.6 0.1 slice_bitcast_fusion.9
  150.7 0.3 fusion.12
  151.0 0.1 copy.137
  151.1 0.1 fusion.23
  151.3 0.1 copy.136
  151.4 0.1 fusion.22
  151.5 0.2 pad_maximum_fusion.10
  151.7 0.2 pad_maximum_fusion.11
  151.9 0.4 maximum_bitcast_fusion.3
  152.2 0.1 slice_bitcast_fusion.6
  152.4 0.1 slice_bitcast_fusion.7
  152.5 0.2 pad_maximum_fusion.13
  152.7 0.1 copy.141
  152.8 0.2 pad_maximum_fusion.12
  153.0 0.3 fusion.7
  153.3 0.4 maximum_bitcast_fusion.5
  153.7 0.1 slice_bitcast_fusion.2
  153.7 0.1 slice_bitcast_fusion.3
  153.9 0.3 fusion.11
  154.3 0.1 copy.146
  154.4 0.1 copy.147
  154.5 0.6 fusion.18
  155.1 0.3 pad_maximum_fusion.1
  155.5 0.2 slice_minimum_fusion.1
  155.7 0.3 pad_maximum_fusion.2
  156.1 0.2 slice_maximum_fusion
  156.3 0.3 convert_reduce_fusion
  156.6 0.3 pad_maximum_fusion
  157.0 0.1 fusion.20
  157.0 0.8 pad_maximum_fusion.16
  157.9 56.9 %all-gather.2.cloned.1.call-done = bf16[128,28672]{1,0:T(8,128)(2,1)} async-done(((bf16[8,28672]{1,0:T(8,128)(2,1)}), bf16[128,28672]{1,0:T(8,128)(2,1)}) %all-gather.2.cloned.1.call-update) | async-done | bytes 7340048 | tf_op jit(solution)/shard_map/all_gather | solution.py:30
  214.7 7.0 %fusion.21 = (bf16[128,14336]{1,0:T(8,128)(2,1)}, bf16[128,14336]{1,0:T(8,128)(2,1)}) fusion(bf16[128,28672]{1,0:T(8,128)(2,1)} %all-gather.2.cloned.1.call-done), kind=kLoop, calls=%fused_computation.81 | loop fusion | bytes 14680064 | tf_op jit(solution)/shard_map/slice | solution.py:32
  (6 shorter events, 0.2 us)
Async XLA Ops:
  12.9 43.8 %all-to-all-start.1 = ((f32[16,1,1]{2,1,0:T(1,128)}), f32[16,1,1]{2,1,0:T(1,128)S(1)}, u32[]{:S(2)}, u32[]{:S(2)}) async-start(f32[16,1,1]{2,1,0:T(1,128)} %broadcast_in_dim.4), calls=%async_computation.1 | async-start | bytes 16384 | tf_op jit(solution)/shard_map/all_to_all | solution.py:9
  58.6 17.1 %all-to-all-start.2 = ((f32[16,1,1]{2,1,0:T(1,128)}), f32[16,1,1]{2,1,0:T(1,128)S(1)}, u32[]{:S(2)}, u32[]{:S(2)}) async-start(f32[16,1,1]{2,1,0:T(1,128)} %broadcast_in_dim.5), calls=%async_computation.2 | async-start | bytes 16384 | tf_op jit(solution)/shard_map/all_to_all | solution.py:9
  75.7 54.2 %all-to-all-start = ((bf16[16,2,57344]{2,1,0:T(2,128)(2,1)}), bf16[16,2,57344]{2,1,0:T(2,128)(2,1)}, u32[]{:S(2)}, u32[]{:S(2)}) async-start(bf16[16,2,57344]{2,1,0:T(2,128)(2,1)} %reshape.391), calls=%async_computation | async-start | bytes 7340032 | tf_op jit(solution)/shard_map/all_to_all | solution.py:85
  81.4 133.3 %all-gather.2.cloned.1.call-start = ((), (), s32[]{:S(2)}) async-start(), calls=%async_computation.3 | async-start | bytes 7798784 | tf_op jit(solution)/shard_map/all_gather | solution.py:30
Sparse Core Ops, SparseCore 0:
  158.0 56.7 all-gather.1
where the time goes:
time: 229 us
  waiting for transfers between devices  105 us (46%)
  local copies, waits for them, and re-layouts  48.4 us (21%)
  other arithmetic  37.2 us (16%)
  starting transfers between devices  23 us (10%)
  between operations  15.1 us (7%)
    all_gather x1, waiting for transfers between devices, side_by_side(): lax.all_gather(both, axis, axis=dim, tiled=True)  56.9 us
    all_to_all x1, waiting for transfers between devices, shards(): lax.all_to_all(grad, 'worker', split_axis=1, concat_axis=0, tiled=True)  48 us
    unnamed x6, local copies, waits for them, and re-layouts  32.3 us
    unnamed x1, other arithmetic  23.8 us
    all_to_all x2, starting transfers between devices, from_everyone(): lax.all_to_all(jnp.broadcast_to(array[None], (count, *array.shape)), axis...  17 us
    slice x1, local copies, waits for them, and re-layouts, side_by_side(): lax.slice_in_dim(result, at, at + a.shape[along], axis=along)  6.97 us
    all_to_all x1, starting transfers between devices, shards(): lax.all_to_all(grad, 'worker', split_axis=1, concat_axis=0, tiled=True)  5.72 us
    all_to_all x1, local copies, waits for them, and re-layouts, shards(): lax.all_to_all(grad, 'worker', split_axis=1, concat_axis=0, tiled=True)  5.15 us
  transfers between devices with their start and end apart: 4, of which 2 were waited for; matrix products, arithmetic and copies ran while one was open for 19% of the time, Pallas kernels for 0%

commit v1 on v0

v1 whole, which is shorter than its diff:
```python
import functools

import jax
import jax.numpy as jnp
from jax import lax
from jax.experimental import pallas as pl
from jax.experimental.pallas import tpu as pltpu
from jax.sharding import PartitionSpec as P


SORT8 = (
    (0, 1), (2, 3), (4, 5), (6, 7),
    (0, 2), (1, 3), (4, 6), (5, 7),
    (1, 2), (5, 6),
    (0, 4), (1, 5), (2, 6), (3, 7),
    (2, 4), (3, 5),
    (1, 2), (3, 4), (5, 6),
)


def sort8(values):
    values = list(values)
    for low, high in SORT8:
        a, b = values[low], values[high]
        values[low], values[high] = jnp.minimum(a, b), jnp.maximum(a, b)
    return values


def middle(values):
    left, right = sort8(values[:8]), sort8(values[8:])
    lower = [jnp.minimum(left[i], right[7 - i]) for i in range(8)]
    upper = [jnp.maximum(left[i], right[7 - i]) for i in range(8)]
    lower = [jnp.maximum(lower[i], lower[i + 4]) for i in range(4)]
    upper = [jnp.minimum(upper[i], upper[i + 4]) for i in range(4)]
    seventh = jnp.maximum(jnp.maximum(lower[0], lower[1]), jnp.maximum(lower[2], lower[3]))
    eighth = jnp.minimum(jnp.minimum(upper[0], upper[1]), jnp.minimum(upper[2], upper[3]))
    kept = [v.astype(jnp.float32) for v in lower + upper]
    while len(kept) > 1:
        kept = [a + b for a, b in zip(kept[::2], kept[1::2])]
    return seventh.astype(jnp.float32), eighth.astype(jnp.float32), kept[0]


def aggregate_kernel(factor_ref, copies_ref, median_ref, trimmed_ref, *, lanes):
    workers, rows, columns = copies_ref.shape

    def step(i, carry):
        at = pl.ds(pl.multiple_of(i * lanes, lanes), lanes)
        scaled = [
            (copies_ref[w, :, at].astype(jnp.float32) * factor_ref[w]).astype(jnp.bfloat16)
            for w in range(workers)
        ]
        seventh, eighth, total = middle(scaled)
        median_ref[:, at] = ((seventh + eighth) * 0.5).astype(jnp.bfloat16)
        trimmed_ref[:, at] = (total * 0.125).astype(jnp.bfloat16)
        return carry

    lax.fori_loop(0, columns // lanes, step, 0)


def aggregate(copies, factors):
    workers, rows, columns = copies.shape
    block = columns // 7
    out = jax.ShapeDtypeStruct((rows, columns), jnp.bfloat16)
    return pl.pallas_call(
        functools.partial(aggregate_kernel, lanes=256),
        grid=(columns // block,),
        in_specs=[
            pl.BlockSpec(memory_space=pltpu.SMEM),
            pl.BlockSpec((workers, rows, block), lambda i: (0, 0, i)),
        ],
        out_specs=[pl.BlockSpec((rows, block), lambda i: (0, i))] * 2,
        out_shape=[out, out],
        cost_estimate=pl.CostEstimate(
            flops=workers * rows * columns * 8, bytes_accessed=workers * rows * columns * 2, transcendentals=0
        ),
        name="aggregate",
    )(factors, copies)


def shards(grad):
    _, rows, columns = grad.shape
    workers = lax.axis_size("worker")
    pieces = grad.reshape(workers, rows // workers, columns)
    copies = lax.all_to_all(pieces, "worker", 0, 0, tiled=True)
    power = lax.psum(jnp.sum(jnp.square(grad.astype(jnp.float32))), "mp")
    factor = lax.rsqrt(power / (rows * lax.axis_size("mp") * columns) + 0.25)
    factors = lax.all_gather(factor, "worker")
    median, trimmed = aggregate(copies, factors)
    return tuple(lax.all_gather(a, "worker", axis=0, tiled=True) for a in (median, trimmed))


def solution(mesh):
    return jax.shard_map(
        shards,
        mesh=mesh,
        in_specs=(P("worker", "mp", None),),
        out_specs=(P("mp", None), P("mp", None)),
        check_vma=False,
    )
```

time: 229 us -> 190 us (0.83)
  blocking collectives: 0 us -> 72.5 us
  local copies, waits for them, and re-layouts: 48.4 us -> 7.53 us
  other arithmetic: 37.2 us -> 4.54 us
  waiting for transfers between devices: 105 us -> 76.2 us
  starting transfers between devices: 23 us -> 7.54 us
  Pallas kernels: 0 us -> 6.81 us
    all_to_all x3 -> x1, waiting for transfers between devices: 48 us -> 0.01 us  [shards(): copies = lax.all_to_all(pieces, 'worker', 0, 0, tiled=True)]
    psum x0 -> x1, blocking collectives: none -> 38.6 us  [shards(): power = lax.psum(jnp.sum(jnp.square(grad.astype(jnp.float32))), 'mp')]
    unnamed x0 -> x1, blocking collectives: none -> 33.9 us
    unnamed x6 -> x9, local copies, waits for them, and re-layouts: 32.3 us -> 7.53 us
    unnamed x1 -> x0, other arithmetic: 23.8 us -> none
    all_gather x1 -> x2, waiting for transfers between devices: 56.9 us -> 75.5 us  [shards(): lax.all_gather(a, 'worker', axis=0, tiled=True)]
    all_to_all x3 -> x1, starting transfers between devices: 22.8 us -> 7.45 us  [shards(): copies = lax.all_to_all(pieces, 'worker', 0, 0, tiled=True)]
    slice x4 -> x0, local copies, waits for them, and re-layouts: 7.46 us -> none  [the longest x1 6.97 us: side_by_side(): lax.slice_in_dim(result, at, at + a.shape[along], axis=along)]
  transfers between devices with their start and end apart: 4 -> 3, of which waited for: 2 -> 2; matrix products, arithmetic and copies ran while one was open for 19% -> 3% of each run, Pallas kernels for 0% -> 0%
where the time goes in v1:
time: 190 us
  waiting for transfers between devices  76.2 us (40%)
  blocking collectives  72.5 us (38%)
  between operations  14.7 us (8%)
  starting transfers between devices  7.54 us (4%)
  local copies, waits for them, and re-layouts  7.53 us (4%)
  Pallas kernels  6.81 us (4%)
  other arithmetic  4.54 us (2%)
    all_gather x2, waiting for transfers between devices, shards(): lax.all_gather(a, 'worker', axis=0, tiled=True)  75.5 us
    psum x1, blocking collectives, shards(): power = lax.psum(jnp.sum(jnp.square(grad.astype(jnp.float32))), 'mp')  38.6 us
    unnamed x1, blocking collectives  33.9 us
    unnamed x9, local copies, waits for them, and re-layouts  7.53 us
    all_to_all x1, starting transfers between devices, shards(): copies = lax.all_to_all(pieces, 'worker', 0, 0, tiled=True)  7.45 us
    pallas_call x1, Pallas kernels, aggregate(): pl.pallas_call(functools.partial(aggregate_kernel, lanes=256), grid=(colu...  6.81 us
    reduce_sum x1, other arithmetic, shards(): power = lax.psum(jnp.sum(jnp.square(grad.astype(jnp.float32))), 'mp')  4.54 us
  transfers between devices with their start and end apart: 3, of which 2 were waited for; matrix products, arithmetic and copies ran while one was open for 3% of the time, Pallas kernels for 0%

profile of v1, /device:TPU:1, one launch (start us, length us, event | category | flops | bytes accessed | tf_op | source)
XLA Modules:
  0.0 189.8 jit_solution(1858982506576344464)
XLA Ops:
  7.2 7.5 %all-to-all-start = ((bf16[16,8,14336]{2,1,0:T(8,128)(2,1)}), bf16[16,8,14336]{2,1,0:T(8,128)(2,1)}, u32[]{:S(2)}, u32[]{:S(2)}) async-start(bf16[16,8,14336]{2,1,0:T(8,128)(2,1)} %bitcast.3), calls=%async_computation | async-start | bytes 7340032 | tf_op jit(solution)/shard_map/all_to_all | solution.py:84
  14.6 0.0 copy-start.1
  14.6 0.0 all-gather.3.cloned.1.call-start
  14.7 4.5 %multiply_reduce_fusion = f32[]{:T(128)} fusion(bf16[1,128,14336]{2,1,0:T(8,128)(2,1)} %param.1), kind=kLoop, calls=%fused_computation | loop fusion | flops 5505023 | bytes 3670020 | tf_op jit(solution)/shard_map/reduce_sum | solution.py:85
  19.2 38.6 %psum.7 = f32[]{:T(128)} all-reduce(f32[]{:T(128)} %multiply_reduce_fusion), channel_id=1, replica_groups=mesh['worker'=16,'mp'=16] {'mp'}, use_global_device_ids=true, to_apply=%region_1.0 | all-reduce | flops 1 | bytes 8 | tf_op jit(solution)/shard_map/psum | solution.py:85
  58.5 0.0 copy-done.1
  58.5 0.6 dynamic-slice
  59.1 0.8 dynamic-update-slice
  59.9 33.9 %all-reduce.factor_ref = f32[16]{0:T(128)} all-reduce(f32[16]{0:T(128)S(1)} %dynamic-update-slice), channel_id=1, replica_groups=mesh['worker'=16,'mp'=16] {'worker'}, use_global_device_ids=true, to_apply=%add | all-reduce | flops 16 | bytes 128
  93.8 0.0 all-to-all-done.copies_ref
  93.8 6.8 %aggregate.1 = (bf16[8,14336]{1,0:T(8,128)(2,1)}, bf16[8,14336]{1,0:T(8,128)(2,1)}) custom-call(f32[16]{0:T(128)} %all-reduce.factor_ref, bf16[16,8,14336]{2,1,0:T(8,128)(2,1)} %all-to-all-done.copies_ref), custom_call_target="tpu_custom_call" | custom-call | flops 14680064 | bytes 3670016 | tf_op jit(solution)/shard_map/aggregate/pallas_call | solution.py:64
  100.6 0.0 all-gather.3.cloned.1.call-update
  100.6 0.0 all-gather.5.cloned.1.call-start
  100.7 0.7 all-gather.5.cloned.1.call-update
  101.4 33.9 %all-gather.3.cloned.1.call-done = bf16[128,14336]{1,0:T(8,128)(2,1)} async-done(((bf16[8,14336]{1,0:T(8,128)(2,1)}), bf16[128,14336]{1,0:T(8,128)(2,1)}) %all-gather.3.cloned.1.call-update) | async-done | bytes 3670032 | tf_op jit(solution)/shard_map/all_gather | solution.py:89
  135.3 41.6 %all-gather.5.cloned.1.call-done = bf16[128,14336]{1,0:T(8,128)(2,1)} async-done(((bf16[8,14336]{1,0:T(8,128)(2,1)}), bf16[128,14336]{1,0:T(8,128)(2,1)}) %all-gather.5.cloned.1.call-update) | async-done | bytes 3670032 | tf_op jit(solution)/shard_map/all_gather | solution.py:89
  176.8 0.0 copy-start
  176.8 4.3 %copy.6 = bf16[128,14336]{1,0:T(8,128)(2,1)} copy(bf16[128,14336]{1,0:T(8,128)(2,1)} %all-gather.3.cloned.1.call-done) | data formatting | bytes 7340032
  181.2 0.0 copy-done
  181.2 1.8 copy.7
  (1 shorter events, 0.0 us)
Async XLA Ops:
  7.2 86.6 %all-to-all-start = ((bf16[16,8,14336]{2,1,0:T(8,128)(2,1)}), bf16[16,8,14336]{2,1,0:T(8,128)(2,1)}, u32[]{:S(2)}, u32[]{:S(2)}) async-start(bf16[16,8,14336]{2,1,0:T(8,128)(2,1)} %bitcast.3), calls=%async_computation | async-start | bytes 7340032 | tf_op jit(solution)/shard_map/all_to_all | solution.py:84
  14.6 43.9 %copy-start.1 = (u32[256]{0:T(256)S(1)}, u32[256]{0:T(256)}, u32[]{:S(2)}) copy-start(u32[256]{0:T(256)} %constant.10) | copy-start | bytes 3076
  14.6 120.6 %all-gather.3.cloned.1.call-start = ((), (), s32[]{:S(2)}) async-start(), calls=%async_computation.1 | async-start | bytes 3899392 | tf_op jit(solution)/shard_map/all_gather | solution.py:89
  100.6 76.2 %all-gather.5.cloned.1.call-start = ((), (), s32[]{:S(2)}) async-start(), calls=%async_computation.2 | async-start | bytes 3899392 | tf_op jit(solution)/shard_map/all_gather | solution.py:89
  176.8 4.4 %copy-start = (bf16[128,14336]{1,0:T(8,128)(2,1)S(1)}, bf16[128,14336]{1,0:T(8,128)(2,1)}, u32[]{:S(2)}) copy-start(bf16[128,14336]{1,0:T(8,128)(2,1)} %all-gather.5.cloned.1.call-done) | copy-start | bytes 11010052
Sparse Core Ops, SparseCore 0:
  100.7 34.4 all-gather.2
  137.7 39.0 all-gather.4
